TPU v7x, 32 devices: a whole 2x2x4 slice. The times are simulated.
32 devices in a mesh: dp: 8 (over z, x), mp: 4 (over y, core).
Axes of the slice: x: 2, y: 2, z: 4, core: 2. Of those that a mesh axis runs over, the one named last changes fastest.
Arguments:
- teacher_states: bfloat16 [512, 128, 4096], P('dp', None, 'mp'), may hold values from -6 to 6
- teacher_gain: float32 [4096], P('mp'), may hold values from 0.25 to 1.75
- teacher_proj: bfloat16 [4096, 1024], P('mp'), may hold values from -0.09375 to 0.09375
- teacher_mask: int32 [512, 128], P('dp'), may hold values 0 or 1
- student_states: bfloat16 [1024, 64, 768], P(('dp', 'mp')), may hold values from -6 to 6
- student_gain: float32 [768], replicated, may hold values from 0.25 to 1.75
- student_proj: bfloat16 [768, 1024], replicated, may hold values from -0.21875 to 0.21875
- student_mask: int32 [1024, 64], P(('dp', 'mp')), may hold values 0 or 1
- positive: int32 [1024], P(('dp', 'mp')), may hold values from 0 to 511
Outputs:
- grad_embed: float32 [1024, 1024], P(('dp', 'mp'))
- grad_states: bfloat16 [1024, 64, 768], P(('dp', 'mp'))
All inputs are finite; a program needn't handle non-finite values. No bound on the sum of `teacher_mask` or of `student_mask` on one device may be relied on, other than what follows from the above.
Results may differ from a plain program's by a relative error of at most 0.0085.
Values may be sent and summed in bfloat16 or wider, within the bound.
A program may use at most 128 MiB of HBM per device.

v0:
```python
import jax
import jax.numpy as jnp
from jax import lax
from jax.sharding import PartitionSpec as P

D = 4096


def unit_rows(values):
    return (
        values
        * lax.rsqrt(jnp.mean(values * values, axis=-1, keepdims=True) + 1e-06)
        / jnp.sqrt(jnp.float32(values.shape[-1]))
    )


def student_forward(states, gain, proj, live_mask):
    values = states.astype(jnp.float32)
    scale = lax.rsqrt(jnp.mean(values * values, axis=-1, keepdims=True) + 1e-06)
    normed = (values * scale * gain).astype(jnp.bfloat16)
    flat = normed.reshape(-1, normed.shape[-1])
    act = jax.nn.gelu(jnp.dot(flat, proj, preferred_element_type=jnp.float32), approximate=True)
    act = act.reshape(states.shape[0], states.shape[1], -1)
    live = live_mask.astype(jnp.float32)
    pooled = jnp.sum(act * live[:, :, None], axis=1)
    return unit_rows(pooled)


def shards(
    teacher_states,
    teacher_gain,
    teacher_proj,
    teacher_mask,
    student_states,
    student_gain,
    student_proj,
    student_mask,
    positive,
):
    values = teacher_states.astype(jnp.float32)
    partial_squares = jnp.sum(values * values, axis=-1)
    squares = lax.psum(partial_squares, "mp")
    scale = lax.rsqrt(squares / D + 1e-06)
    live = teacher_mask.astype(jnp.float32)
    weight = live * scale
    pooled = jnp.sum(values * weight[:, :, None], axis=1)
    tpooled = (pooled * teacher_gain).astype(jnp.bfloat16)
    partial_embed = jnp.dot(tpooled, teacher_proj, preferred_element_type=jnp.float32)
    summed = lax.psum(partial_embed, "mp")
    group_emb = unit_rows(summed).astype(jnp.bfloat16)
    gathered = lax.all_gather(group_emb, "dp", axis=0, tiled=True)
    semb, back = jax.vjp(
        lambda st: student_forward(st, student_gain, student_proj, student_mask), student_states
    )
    sround = semb.astype(jnp.bfloat16)
    columns = lax.broadcasted_iota(jnp.int32, (positive.shape[0], gathered.shape[0]), 1)
    picker = (positive[:, None] == columns).astype(jnp.bfloat16)
    tpos = jnp.dot(picker, gathered, preferred_element_type=jnp.float32).astype(jnp.bfloat16)
    tlogit = 10.0 * jnp.dot(tpos, gathered.T, preferred_element_type=jnp.float32)
    slogit = 20.0 * jnp.dot(sround, gathered.T, preferred_element_type=jnp.float32)
    texp = jnp.exp(tlogit)
    sexp = jnp.exp(slogit)
    diff = (
        sexp / jnp.sum(sexp, axis=1, keepdims=True) - texp / jnp.sum(texp, axis=1, keepdims=True)
    ).astype(jnp.bfloat16)
    grad_embed = 20.0 * jnp.dot(diff, gathered, preferred_element_type=jnp.float32)
    grad_states = back(grad_embed)[0]
    return (grad_embed, grad_states)


def solution(mesh):
    in_specs = (
        P("dp", None, "mp"),
        P("mp"),
        P("mp", None),
        P("dp", None),
        P(("dp", "mp"), None, None),
        P(),
        P(),
        P(("dp", "mp"), None),
        P(("dp", "mp")),
    )
    out_specs = (P(("dp", "mp"), None), P(("dp", "mp"), None, None))
    return jax.shard_map(shards, mesh=mesh, in_specs=in_specs, out_specs=out_specs, check_vma=False)
```

profile of v0, /device:TPU:0, one launch (start us, length us, event | category | flops | bytes accessed | tf_op | source)
XLA Modules:
  0.0 156.2 jit_solution(10778247551571147130)
XLA Ops:
  7.2 0.0 copy-start
  7.2 0.0 copy-start.6
  7.2 0.0 all-reduce.2.cloned.1.call-start
  7.2 7.4 %fusion = f32[64,128]{1,0:T(8,128)S(1)} fusion(bf16[64,128,1024]{2,1,0:T(8,128)(2,1)} %param.9), kind=kLoop, calls=%fused_computation.2 | loop fusion | flops 25157632 | bytes 16809984 | tf_op jit(solution)/shard_map/reduce_sum | solution.py:41
  14.6 12.9 %psum.14 = f32[64,128]{1,0:T(8,128)S(1)} all-reduce(f32[64,128]{1,0:T(8,128)S(1)} %fusion), channel_id=1, replica_groups=mesh['dp'=8,'mp'=4] {'mp'}, use_global_device_ids=true, to_apply=%region_4.0 | all-reduce | flops 8192 | bytes 65536 | tf_op jit(solution)/shard_map/psum | solution.py:42
  27.6 0.0 copy-done.6
  27.6 0.0 copy-start.8
  27.6 0.0 copy-start.7
  27.6 0.0 copy-start.5
  27.6 7.6 %fusion.1 = f32[64,1024]{1,0:T(8,128)S(1)} fusion(bf16[64,128,1024]{2,1,0:T(8,128)(2,1)} %param.9, f32[64,128]{1,0:T(8,128)S(1)} %rsqrt_multiply_fusion), kind=kLoop, calls=%fused_computation.3 | loop fusion | flops 25100288 | bytes 17072128 | tf_op jit(solution)/shard_map/reduce_sum | solution.py:46
  35.3 0.0 copy-done
  35.3 0.0 copy-done.8
  35.3 1.2 fusion.31
  36.5 0.0 all-reduce.2.cloned.1.call-update
  36.5 0.0 all-gather.2.cloned.1.call-start
  36.6 32.7 %all-reduce.2.cloned.1.call-done = f32[64,1024]{1,0:T(8,128)} async-done(((f32[64,1024]{1,0:T(8,128)}), f32[64,1024]{1,0:T(8,128)}) %all-reduce.2.cloned.1.call-update) | async-done | bytes 262160 | tf_op jit(solution)/shard_map/psum | solution.py:49
  69.2 1.1 multiply_reduce_fusion.1
  70.3 1.7 %multiply_convert_fusion = bf16[64,1024]{1,0:T(8,128)(2,1)} fusion(f32[64,1024]{1,0:T(8,128)} %all-reduce.2.cloned.1.call-done, f32[64]{0:T(128)S(1)} %add_rsqrt_fusion), kind=kLoop, calls=%fused_computation.43 | loop fusion | flops 196608 | bytes 393472 | tf_op jit(solution)/shard_map/convert_element_type | solution.py:50
  72.0 0.0 all-gather.2.cloned.1.call-update
  72.1 0.0 copy-done.7
  72.1 0.1 mul.250
  72.2 0.0 copy-start.3
  72.2 2.7 %fusion.17 = f32[32,64]{1,0:T(8,128)S(1)} fusion(bf16[32,64,768]{2,1,0:T(8,128)(2,1)} %param.13), kind=kLoop, calls=%fused_computation.28 | loop fusion | flops 4716544 | bytes 3153920 | tf_op jit(solution)/shard_map/jvp()/reduce_sum | solution.py:19
  74.9 0.0 copy-done.5
  74.9 0.0 copy-start.9
  74.9 2.7 %fusion.19 = bf16[32,64,768]{2,1,0:T(8,128)(2,1)S(1)} fusion(bf16[32,64,768]{2,1,0:T(8,128)(2,1)} %param.13, f32[768]{0:T(1024)S(1)} %copy-done.5, f32[32,64]{1,0:T(8,128)S(1)} %fusion.40), kind=kLoop, calls=%fused_computation.30 | loop fusion | flops 6291456 | bytes 6302720 | tf_op jit(solution)/shard_map/jvp()/convert_element_type | solution.py:20
  77.6 0.0 copy-done.3
  77.6 7.7 %multiply_reduce_fusion = (f32[32,1024]{1,0:T(8,128)S(1)}, f32[2048,1024]{1,0:T(8,128)}) fusion(f32[32,64]{1,0:T(8,128)S(1)} %convert_element_type.45, bf16[2048,768]{1,0:T(8,128)(2,1)S(1)} %bitcast.31, bf16[768,1024]{1,0:T(8,128)(2,1)S(1)} %copy-done.3), kind=kOutput, calls=%fused_computation.25 | convolution fusion | flops 3242164224 | bytes 13246464 | tf_op jit(solution)/shard_map/jvp()/dot_general | solution.py:22
  85.3 0.1 multiply_reduce_fusion.3
  85.4 27.1 %all-gather.2.cloned.1.call-done = bf16[512,1024]{1,0:T(8,128)(2,1)} async-done(((bf16[64,1024]{1,0:T(8,128)(2,1)}), bf16[512,1024]{1,0:T(8,128)(2,1)}) %all-gather.2.cloned.1.call-update) | async-done | bytes 1048592 | tf_op jit(solution)/shard_map/all_gather | solution.py:51
  112.5 0.0 copy-done.9
  112.5 2.5 %fusion.45 = (f32[32]{0:T(128)S(1)}, f32[32,512]{1,0:T(8,128)S(1)}) fusion(bf16[512,1024]{1,0:T(8,128)(2,1)} %all-gather.2.cloned.1.call-done, s32[32]{0:T(128)S(1)} %copy-done.9), kind=kOutput, calls=%fused_computation.73 | convolution fusion | flops 67190752 | bytes 1114368 | tf_op jit(solution)/shard_map/dot_general | solution.py:59
  115.0 1.8 %fusion.46 = (f32[32]{0:T(128)S(1)}, f32[32,512]{1,0:T(8,128)S(1)}) fusion(bf16[512,1024]{1,0:T(8,128)(2,1)} %all-gather.2.cloned.1.call-done, f32[32,1024]{1,0:T(8,128)S(1)} %get-tuple-element.8, f32[32]{0:T(128)S(1)} %fusion.41), kind=kOutput, calls=%fused_computation.74 | convolution fusion | flops 33685472 | bytes 1245440 | tf_op jit(solution)/shard_map/dot_general | solution.py:60
  116.7 1.7 %multiply_reduce_fusion.2 = (f32[32]{0:T(128)S(1)}, f32[32,1024]{1,0:T(8,128)S(1)}) fusion(f32[32,1024]{1,0:T(8,128)S(1)} %get-tuple-element.8, bf16[512,1024]{1,0:T(8,128)(2,1)} %all-gather.2.cloned.1.call-done, f32[32,512]{1,0:T(8,128)S(1)} %get-tuple-element.11, f32[32,512]{1,0:T(8,128)S(1)} %get-tuple-element.13, f32[32]{0:T(128)S(1)} %get-tuple-element.10, ...), kind=kOutput, calls=%fused_computation.48 | convolution fusion | flops 33718240 | bytes 1442176 | tf_op jit(solution)/shard_map/dot_general | solution.py:66
  118.4 0.0 slice-start
  118.4 0.7 add_add_fusion.1
  119.1 0.0 slice-start.1
  119.1 0.0 copy-start.4
  119.1 11.1 %fusion.14 = (f32[2048,1024]{1,0:T(8,128)}, f32[2048,1024]{1,0:T(8,128)}) fusion(f32[2048,1024]{1,0:T(8,128)} %get-tuple-element.9, f32[2048]{0:T(1024)S(1)} %mul.250, f32[32,1024]{1,0:T(8,128)S(1)} %get-tuple-element.4), kind=kLoop, calls=%fused_computation.23 | loop fusion | flops 33554432 | bytes 25305088 | tf_op jit(solution)/shard_map/transpose(jvp())/mul | solution.py:22
  130.2 0.0 slice-done
  130.2 0.0 slice-done.1
  130.2 0.0 copy-done.4
  130.2 11.6 %fusion.24 = bf16[2048,768]{1,0:T(8,128)(2,1)} fusion(bf16[768,1024]{1,0:T(8,128)(2,1)S(1)} %copy-done.4, f32[2048,1024]{1,0:T(8,128)} %get-tuple-element.3, f32[2048,1024]{1,0:T(8,128)S(1)} %bitcast.29, f32[2048,1024]{1,0:T(8,128)} %get-tuple-element.2), kind=kOutput, calls=%fused_computation.36 | convolution fusion | flops 3233284096 | bytes 29884416 | tf_op jit(solution)/shard_map/transpose(jvp())/dot_general | solution.py:22
  141.9 0.0 copy-start.1
  141.9 0.0 copy-start.2
  141.9 4.1 %fusion.20 = f32[32,64]{1,0:T(8,128)S(1)} fusion(bf16[32,64,768]{2,1,0:T(8,128)(2,1)} %param.13, bf16[32,64,768]{2,1,0:T(8,128)(2,1)} %bitcast.30, f32[768]{0:T(1024)S(1)} %copy-done.5), kind=kLoop, calls=%fused_computation.31 | loop fusion | flops 7862272 | bytes 6302720 | tf_op jit(solution)/shard_map/transpose(jvp())/reduce_sum | solution.py:20
  146.0 0.0 copy-done.1
  146.0 0.6 copy-done.2
  146.6 2.8 %fusion.16 = bf16[32,64,768]{2,1,0:T(8,128)(2,1)} fusion(bf16[32,64,768]{2,1,0:T(8,128)(2,1)S(1)} %copy-done.1, f32[32,64]{1,0:T(8,128)S(1)} %multiply_multiply_fusion.3, f32[768]{0:T(1024)S(1)} %copy-done.5, f32[32,64]{1,0:T(8,128)S(1)} %fusion.40, bf16[2048,768]{1,0:T(8,128)(2,1)S(1)} %copy-done.2), kind=kLoop, calls=%fused_computation.27 | loop fusion | flops 12582912 | bytes 9456640 | tf_op jit(solution)/shard_map/transpose(jvp())/convert_element_type | solution.py:18
  (8 shorter events, 0.1 us)
Async XLA Ops:
  7.2 28.1 %copy-start = (bf16[1024,1024]{1,0:T(8,128)(2,1)S(1)}, bf16[1024,1024]{1,0:T(8,128)(2,1)}, u32[]{:S(2)}) copy-start(bf16[1024,1024]{1,0:T(8,128)(2,1)} %param.11) | copy-start | bytes 6291460
  7.2 20.4 %copy-start.6 = (s32[64,128]{1,0:T(8,128)S(1)}, s32[64,128]{1,0:T(8,128)}, u32[]{:S(2)}) copy-start(s32[64,128]{1,0:T(8,128)} %param.12) | copy-start | bytes 98308
  7.2 62.1 %all-reduce.2.cloned.1.call-start = ((), (), s32[]{:S(2)}) async-start(), calls=%async_computation | async-start | bytes 524288 | tf_op jit(solution)/shard_map/psum | solution.py:49
  27.6 7.7 %copy-start.8 = (f32[1024]{0:T(1024)S(1)}, f32[1024]{0:T(1024)}, u32[]{:S(2)}) copy-start(f32[1024]{0:T(1024)} %param.10) | copy-start | bytes 12292
  27.6 44.5 %copy-start.7 = (s32[32,64]{1,0:T(8,128)S(1)}, s32[32,64]{1,0:T(8,128)}, u32[]{:S(2)}) copy-start(s32[32,64]{1,0:T(8,128)} %param.16) | copy-start | bytes 24580
  27.6 47.2 %copy-start.5 = (f32[768]{0:T(1024)S(1)}, f32[768]{0:T(1024)}, u32[]{:S(2)}) copy-start(f32[768]{0:T(1024)} %param.14) | copy-start | bytes 9220
  36.5 76.0 %all-gather.2.cloned.1.call-start = ((), (), s32[]{:S(2)}) async-start(), calls=%async_computation.1 | async-start | bytes 1179648 | tf_op jit(solution)/shard_map/all_gather | solution.py:51
  72.2 5.4 %copy-start.3 = (bf16[768,1024]{1,0:T(8,128)(2,1)S(1)}, bf16[768,1024]{1,0:T(8,128)(2,1)}, u32[]{:S(2)}) copy-start(bf16[768,1024]{1,0:T(8,128)(2,1)} %param.15) | copy-start | bytes 4718596
  74.9 37.6 %copy-start.9 = (s32[32]{0:T(128)S(1)}, s32[32]{0:T(128)}, u32[]{:S(2)}) copy-start(s32[32]{0:T(128)} %param.17) | copy-start | bytes 388
  118.4 11.8 %slice-start = ((s8[8388608]{0:T(1024)(128)(4,1)}), s8[4194304]{0:T(1024)(128)(4,1)S(1)}, s32[]{:S(2)}) async-start(s8[8388608]{0:T(1024)(128)(4,1)} %bitcast.28), calls=%async_computation.2 | async-start | bytes 8388608
  119.1 11.1 %slice-start.1 = ((s8[8388608]{0:T(1024)(128)(4,1)}), s8[4194304]{0:T(1024)(128)(4,1)S(1)}, s32[]{:S(2)}) async-start(s8[8388608]{0:T(1024)(128)(4,1)} %bitcast.28), calls=%async_computation.3 | async-start | bytes 8388608
  119.1 11.1 %copy-start.4 = (bf16[768,1024]{1,0:T(8,128)(2,1)S(1)}, bf16[768,1024]{1,0:T(8,128)(2,1)}, u32[]{:S(2)}) copy-start(bf16[768,1024]{1,0:T(8,128)(2,1)} %param.15) | copy-start | bytes 4718596
  141.9 4.1 %copy-start.1 = (bf16[32,64,768]{2,1,0:T(8,128)(2,1)S(1)}, bf16[32,64,768]{2,1,0:T(8,128)(2,1)}, u32[]{:S(2)}) copy-start(bf16[32,64,768]{2,1,0:T(8,128)(2,1)} %param.13) | copy-start | bytes 9437188
  141.9 4.7 %copy-start.2 = (bf16[2048,768]{1,0:T(8,128)(2,1)S(1)}, bf16[2048,768]{1,0:T(8,128)(2,1)}, u32[]{:S(2)}) copy-start(bf16[2048,768]{1,0:T(8,128)(2,1)} %fusion.24) | copy-start | bytes 9437188
Sparse Core Ops, SparseCore 0:
  36.6 32.5 all-reduce.1
  72.2 40.2 all-gather.1
where the time goes:
time: 157 us; the launch traced here: 156 us
  waiting for transfers between devices  59.8 us (38%)
  other arithmetic  41.9 us (27%)
  matrix products  26.5 us (17%)
  between operations  14.2 us (9%)
  blocking collectives  12.9 us (8%)
    psum x1, waiting for transfers between devices, shards(): summed = lax.psum(partial_embed, 'mp')  32.7 us
    all_gather x1, waiting for transfers between devices, shards(): gathered = lax.all_gather(group_emb, 'dp', axis=0, tiled=True)  27.1 us
    dot_general x2, matrix products, student_forward(): jnp.dot(flat, proj, preferred_element_type=jnp.float32)  19.3 us
    psum x1, blocking collectives, shards(): squares = lax.psum(partial_squares, 'mp')  12.9 us
    mul x1, other arithmetic, student_forward(): jax.nn.gelu(jnp.dot(flat, proj, preferred_element_type=jnp.float32), appr...  11.1 us
    reduce_sum x1, other arithmetic, shards(): pooled = jnp.sum(values * weight[:, :, None], axis=1)  7.65 us
    reduce_sum x1, other arithmetic, shards(): partial_squares = jnp.sum(values * values, axis=-1)  7.38 us
    reduce_sum x1, other arithmetic, student_forward(): normed = (values * scale * gain).astype(jnp.bfloat16)  4.07 us
  transfers between devices with their start and end apart: 2, of which 2 were waited for; matrix products, arithmetic and copies ran while one was open for 8% of the time, Pallas kernels for 0%

commit v1 on v0

--- a/solution.py
+++ b/solution.py
@@ -46,7 +46,7 @@
     pooled = jnp.sum(values * weight[:, :, None], axis=1)
     tpooled = (pooled * teacher_gain).astype(jnp.bfloat16)
     partial_embed = jnp.dot(tpooled, teacher_proj, preferred_element_type=jnp.float32)
-    summed = lax.psum(partial_embed, "mp")
+    summed = jnp.sum(lax.all_gather(partial_embed, "mp"), axis=0)
     group_emb = unit_rows(summed).astype(jnp.bfloat16)
     gathered = lax.all_gather(group_emb, "dp", axis=0, tiled=True)
     semb, back = jax.vjp(

time: 157 us -> 141 us (0.90)
  waiting for transfers between devices: 59.8 us -> 44.6 us
    psum x1 -> x0, waiting for transfers between devices: 32.7 us -> none  [shards(): summed = lax.psum(partial_embed, 'mp')]
    all_gather x0 -> x1, waiting for transfers between devices: none -> 17.1 us  [shards(): summed = jnp.sum(lax.all_gather(partial_embed, 'mp'), axis=0)]
  transfers between devices with their start and end apart: 2 -> 2, of which waited for: 2 -> 2; matrix products, arithmetic and copies ran while one was open for 8% -> 9% of each run, Pallas kernels for 0% -> 0%
where the time goes in v1:
time: 141 us; the launch traced here: 140 us
  waiting for transfers between devices  44.6 us (32%)
  other arithmetic  41.4 us (29%)
  matrix products  26.4 us (19%)
  between operations  14.2 us (10%)
  blocking collectives  12.9 us (9%)
    all_gather x1, waiting for transfers between devices, shards(): gathered = lax.all_gather(group_emb, 'dp', axis=0, tiled=True)  27.5 us
    dot_general x2, matrix products, student_forward(): jnp.dot(flat, proj, preferred_element_type=jnp.float32)  19.3 us
    all_gather x1, waiting for transfers between devices, shards(): summed = jnp.sum(lax.all_gather(partial_embed, 'mp'), axis=0)  17.1 us
    psum x1, blocking collectives, shards(): squares = lax.psum(partial_squares, 'mp')  12.9 us
    mul x1, other arithmetic, student_forward(): jax.nn.gelu(jnp.dot(flat, proj, preferred_element_type=jnp.float32), appr...  11.1 us
    reduce_sum x1, other arithmetic, shards(): pooled = jnp.sum(values * weight[:, :, None], axis=1)  7.65 us
    reduce_sum x1, other arithmetic, shards(): partial_squares = jnp.sum(values * values, axis=-1)  7.38 us
    reduce_sum x1, other arithmetic, student_forward(): normed = (values * scale * gain).astype(jnp.bfloat16)  4.07 us
  transfers between devices with their start and end apart: 2, of which 2 were waited for; matrix products, arithmetic and copies ran while one was open for 9% of the time, Pallas kernels for 0%

profile of v1, /device:TPU:0, one launch (start us, length us, event | category | flops | bytes accessed | tf_op | source)
XLA Modules:
  0.0 140.4 jit_solution(2609986423839235895)
XLA Ops:
  7.2 0.0 copy-start
  7.2 0.0 copy-start.6
  7.2 0.0 all-gather.6.cloned.1.call-start
  7.2 7.4 %fusion = f32[64,128]{1,0:T(8,128)S(1)} fusion(bf16[64,128,1024]{2,1,0:T(8,128)(2,1)} %param.9), kind=kLoop, calls=%fused_computation.2 | loop fusion | flops 25157632 | bytes 16809984 | tf_op jit(solution)/shard_map/reduce_sum | solution.py:41
  14.6 12.9 %psum.7 = f32[64,128]{1,0:T(8,128)S(1)} all-reduce(f32[64,128]{1,0:T(8,128)S(1)} %fusion), channel_id=1, replica_groups=mesh['dp'=8,'mp'=4] {'mp'}, use_global_device_ids=true, to_apply=%region_4.0 | all-reduce | flops 8192 | bytes 65536 | tf_op jit(solution)/shard_map/psum | solution.py:42
  27.6 0.0 copy-done.6
  27.6 0.0 copy-start.8
  27.6 0.0 copy-start.7
  27.6 0.0 copy-start.5
  27.6 7.6 %fusion.1 = f32[64,1024]{1,0:T(8,128)S(1)} fusion(bf16[64,128,1024]{2,1,0:T(8,128)(2,1)} %param.9, f32[64,128]{1,0:T(8,128)S(1)} %rsqrt_multiply_fusion), kind=kLoop, calls=%fused_computation.3 | loop fusion | flops 25100288 | bytes 17072128 | tf_op jit(solution)/shard_map/reduce_sum | solution.py:46
  35.3 0.0 copy-done
  35.3 0.0 copy-done.8
  35.3 1.2 fusion.31
  36.5 0.0 all-gather.6.cloned.1.call-update
  36.5 0.0 all-gather.4.cloned.1.call-start
  36.6 17.1 %all-gather.6.cloned.1.call-done = f32[256,1024]{1,0:T(8,128)} async-done(((f32[64,1024]{1,0:T(8,128)}), f32[256,1024]{1,0:T(8,128)}) %all-gather.6.cloned.1.call-update) | async-done | bytes 1048592 | tf_op jit(solution)/shard_map/all_gather | solution.py:49
  53.7 1.3 reduce_sum.112
  55.0 0.1 multiply_reduce_fusion.1
  55.1 0.8 multiply_convert_fusion
  55.9 0.0 all-gather.4.cloned.1.call-update
  55.9 0.0 copy-done.7
  55.9 0.1 mul.250
  56.0 0.0 copy-start.3
  56.0 2.7 %fusion.17 = f32[32,64]{1,0:T(8,128)S(1)} fusion(bf16[32,64,768]{2,1,0:T(8,128)(2,1)} %param.13), kind=kLoop, calls=%fused_computation.28 | loop fusion | flops 4716544 | bytes 3153920 | tf_op jit(solution)/shard_map/jvp()/reduce_sum | solution.py:19
  58.7 0.0 copy-done.5
  58.7 0.0 copy-start.9
  58.7 2.7 %fusion.19 = bf16[32,64,768]{2,1,0:T(8,128)(2,1)S(1)} fusion(bf16[32,64,768]{2,1,0:T(8,128)(2,1)} %param.13, f32[768]{0:T(1024)S(1)} %copy-done.5, f32[32,64]{1,0:T(8,128)S(1)} %fusion.40), kind=kLoop, calls=%fused_computation.30 | loop fusion | flops 6291456 | bytes 6302720 | tf_op jit(solution)/shard_map/jvp()/convert_element_type | solution.py:20
  61.4 0.0 copy-done.3
  61.4 7.7 %multiply_reduce_fusion = (f32[32,1024]{1,0:T(8,128)S(1)}, f32[2048,1024]{1,0:T(8,128)}) fusion(f32[32,64]{1,0:T(8,128)S(1)} %convert_element_type.45, bf16[2048,768]{1,0:T(8,128)(2,1)S(1)} %bitcast.32, bf16[768,1024]{1,0:T(8,128)(2,1)S(1)} %copy-done.3), kind=kOutput, calls=%fused_computation.25 | convolution fusion | flops 3242164224 | bytes 13246464 | tf_op jit(solution)/shard_map/jvp()/dot_general | solution.py:22
  69.1 0.1 multiply_reduce_fusion.3
  69.2 27.5 %all-gather.4.cloned.1.call-done = bf16[512,1024]{1,0:T(8,128)(2,1)} async-done(((bf16[64,1024]{1,0:T(8,128)(2,1)}), bf16[512,1024]{1,0:T(8,128)(2,1)}) %all-gather.4.cloned.1.call-update) | async-done | bytes 1048592 | tf_op jit(solution)/shard_map/all_gather | solution.py:51
  96.7 0.0 copy-done.9
  96.7 2.5 %fusion.45 = (f32[32]{0:T(128)S(1)}, f32[32,512]{1,0:T(8,128)S(1)}) fusion(bf16[512,1024]{1,0:T(8,128)(2,1)} %all-gather.4.cloned.1.call-done, s32[32]{0:T(128)S(1)} %copy-done.9), kind=kOutput, calls=%fused_computation.73 | convolution fusion | flops 67190752 | bytes 1114368 | tf_op jit(solution)/shard_map/dot_general | solution.py:59
  99.2 1.8 %fusion.46 = (f32[32]{0:T(128)S(1)}, f32[32,512]{1,0:T(8,128)S(1)}) fusion(bf16[512,1024]{1,0:T(8,128)(2,1)} %all-gather.4.cloned.1.call-done, f32[32,1024]{1,0:T(8,128)S(1)} %get-tuple-element.8, f32[32]{0:T(128)S(1)} %fusion.41), kind=kOutput, calls=%fused_computation.74 | convolution fusion | flops 33685472 | bytes 1245440 | tf_op jit(solution)/shard_map/dot_general | solution.py:60
  100.9 1.7 %multiply_reduce_fusion.2 = (f32[32]{0:T(128)S(1)}, f32[32,1024]{1,0:T(8,128)S(1)}) fusion(f32[32,1024]{1,0:T(8,128)S(1)} %get-tuple-element.8, bf16[512,1024]{1,0:T(8,128)(2,1)} %all-gather.4.cloned.1.call-done, f32[32,512]{1,0:T(8,128)S(1)} %get-tuple-element.11, f32[32,512]{1,0:T(8,128)S(1)} %get-tuple-element.13, f32[32]{0:T(128)S(1)} %get-tuple-element.10, ...), kind=kOutput, calls=%fused_computation.48 | convolution fusion | flops 33718240 | bytes 1442176 | tf_op jit(solution)/shard_map/dot_general | solution.py:66
  102.6 0.0 slice-start
  102.6 0.7 add_add_fusion.1
  103.3 0.0 slice-start.1
  103.3 0.0 copy-start.4
  103.3 11.1 %fusion.14 = (f32[2048,1024]{1,0:T(8,128)}, f32[2048,1024]{1,0:T(8,128)}) fusion(f32[2048,1024]{1,0:T(8,128)} %get-tuple-element.9, f32[2048]{0:T(1024)S(1)} %mul.250, f32[32,1024]{1,0:T(8,128)S(1)} %get-tuple-element.4), kind=kLoop, calls=%fused_computation.23 | loop fusion | flops 33554432 | bytes 25305088 | tf_op jit(solution)/shard_map/transpose(jvp())/mul | solution.py:22
  114.4 0.0 slice-done
  114.4 0.0 slice-done.1
  114.4 0.0 copy-done.4
  114.4 11.6 %fusion.24 = bf16[2048,768]{1,0:T(8,128)(2,1)} fusion(bf16[768,1024]{1,0:T(8,128)(2,1)S(1)} %copy-done.4, f32[2048,1024]{1,0:T(8,128)} %get-tuple-element.3, f32[2048,1024]{1,0:T(8,128)S(1)} %bitcast.30, f32[2048,1024]{1,0:T(8,128)} %get-tuple-element.2), kind=kOutput, calls=%fused_computation.36 | convolution fusion | flops 3233284096 | bytes 29884416 | tf_op jit(solution)/shard_map/transpose(jvp())/dot_general | solution.py:22
  126.1 0.0 copy-start.1
  126.1 0.0 copy-start.2
  126.1 4.1 %fusion.20 = f32[32,64]{1,0:T(8,128)S(1)} fusion(bf16[32,64,768]{2,1,0:T(8,128)(2,1)} %param.13, bf16[32,64,768]{2,1,0:T(8,128)(2,1)} %bitcast.31, f32[768]{0:T(1024)S(1)} %copy-done.5), kind=kLoop, calls=%fused_computation.31 | loop fusion | flops 7862272 | bytes 6302720 | tf_op jit(solution)/shard_map/transpose(jvp())/reduce_sum | solution.py:20
  130.1 0.0 copy-done.1
  130.2 0.6 copy-done.2
  130.8 2.8 %fusion.16 = bf16[32,64,768]{2,1,0:T(8,128)(2,1)} fusion(bf16[32,64,768]{2,1,0:T(8,128)(2,1)S(1)} %copy-done.1, f32[32,64]{1,0:T(8,128)S(1)} %multiply_multiply_fusion.3, f32[768]{0:T(1024)S(1)} %copy-done.5, f32[32,64]{1,0:T(8,128)S(1)} %fusion.40, bf16[2048,768]{1,0:T(8,128)(2,1)S(1)} %copy-done.2), kind=kLoop, calls=%fused_computation.27 | loop fusion | flops 12582912 | bytes 9456640 | tf_op jit(solution)/shard_map/transpose(jvp())/convert_element_type | solution.py:18
  (8 shorter events, 0.1 us)
Async XLA Ops:
  7.2 28.1 %copy-start = (bf16[1024,1024]{1,0:T(8,128)(2,1)S(1)}, bf16[1024,1024]{1,0:T(8,128)(2,1)}, u32[]{:S(2)}) copy-start(bf16[1024,1024]{1,0:T(8,128)(2,1)} %param.11) | copy-start | bytes 6291460
  7.2 20.4 %copy-start.6 = (s32[64,128]{1,0:T(8,128)S(1)}, s32[64,128]{1,0:T(8,128)}, u32[]{:S(2)}) copy-start(s32[64,128]{1,0:T(8,128)} %param.12) | copy-start | bytes 98308
  7.2 46.5 %all-gather.6.cloned.1.call-start = ((), (), s32[]{:S(2)}) async-start(), calls=%async_computation.1 | async-start | bytes 1310720 | tf_op jit(solution)/shard_map/all_gather | solution.py:49
  27.6 7.7 %copy-start.8 = (f32[1024]{0:T(1024)S(1)}, f32[1024]{0:T(1024)}, u32[]{:S(2)}) copy-start(f32[1024]{0:T(1024)} %param.10) | copy-start | bytes 12292
  27.6 28.3 %copy-start.7 = (s32[32,64]{1,0:T(8,128)S(1)}, s32[32,64]{1,0:T(8,128)}, u32[]{:S(2)}) copy-start(s32[32,64]{1,0:T(8,128)} %param.16) | copy-start | bytes 24580
  27.6 31.1 %copy-start.5 = (f32[768]{0:T(1024)S(1)}, f32[768]{0:T(1024)}, u32[]{:S(2)}) copy-start(f32[768]{0:T(1024)} %param.14) | copy-start | bytes 9220
  36.5 60.2 %all-gather.4.cloned.1.call-start = ((), (), s32[]{:S(2)}) async-start(), calls=%async_computation | async-start | bytes 1179648 | tf_op jit(solution)/shard_map/all_gather | solution.py:51
  56.0 5.4 %copy-start.3 = (bf16[768,1024]{1,0:T(8,128)(2,1)S(1)}, bf16[768,1024]{1,0:T(8,128)(2,1)}, u32[]{:S(2)}) copy-start(bf16[768,1024]{1,0:T(8,128)(2,1)} %param.15) | copy-start | bytes 4718596
  58.7 38.0 %copy-start.9 = (s32[32]{0:T(128)S(1)}, s32[32]{0:T(128)}, u32[]{:S(2)}) copy-start(s32[32]{0:T(128)} %param.17) | copy-start | bytes 388
  102.6 11.8 %slice-start = ((s8[8388608]{0:T(1024)(128)(4,1)}), s8[4194304]{0:T(1024)(128)(4,1)S(1)}, s32[]{:S(2)}) async-start(s8[8388608]{0:T(1024)(128)(4,1)} %bitcast.29), calls=%async_computation.2 | async-start | bytes 8388608
  103.3 11.1 %slice-start.1 = ((s8[8388608]{0:T(1024)(128)(4,1)}), s8[4194304]{0:T(1024)(128)(4,1)S(1)}, s32[]{:S(2)}) async-start(s8[8388608]{0:T(1024)(128)(4,1)} %bitcast.29), calls=%async_computation.3 | async-start | bytes 8388608
  103.3 11.1 %copy-start.4 = (bf16[768,1024]{1,0:T(8,128)(2,1)S(1)}, bf16[768,1024]{1,0:T(8,128)(2,1)}, u32[]{:S(2)}) copy-start(bf16[768,1024]{1,0:T(8,128)(2,1)} %param.15) | copy-start | bytes 4718596
  126.1 4.1 %copy-start.1 = (bf16[32,64,768]{2,1,0:T(8,128)(2,1)S(1)}, bf16[32,64,768]{2,1,0:T(8,128)(2,1)}, u32[]{:S(2)}) copy-start(bf16[32,64,768]{2,1,0:T(8,128)(2,1)} %param.13) | copy-start | bytes 9437188
  126.1 4.7 %copy-start.2 = (bf16[2048,768]{1,0:T(8,128)(2,1)S(1)}, bf16[2048,768]{1,0:T(8,128)(2,1)}, u32[]{:S(2)}) copy-start(bf16[2048,768]{1,0:T(8,128)(2,1)} %fusion.24) | copy-start | bytes 9437188
Sparse Core Ops, SparseCore 0:
  36.6 16.9 all-gather.5
  56.4 40.2 all-gather.3
